TPU v7x, 256 devices: a whole 4x4x8 slice. The times are simulated.
256 devices in a mesh: snap: 8 (over z), vert: 32 (over x, y, core).
Axes of the slice: x: 4, y: 4, z: 8, core: 2. Of those that a mesh axis runs over, the one named last changes fastest.
Arguments:
- features: bfloat16 [16, 65536, 256], P('snap', 'vert'), may hold values from -6 to 6
- tile_rows: int32 [16, 2048], P('snap', 'vert'), may hold values from 0 to 15
- tile_cols: int32 [16, 2048], P('snap', 'vert'), may hold values from 0 to 21
- tile_vals: bfloat16 [16, 2048, 128, 128], P('snap', 'vert'), may hold values from -0.25 to 0.25
- send_lists: int32 [32, 6], replicated, may hold values from 0 to 15
- conv1_weight: bfloat16 [256, 256], replicated, may hold values from -0.375 to 0.375
- conv2_weight: bfloat16 [256, 256], replicated, may hold values from -0.375 to 0.375
- lstm_weight: bfloat16 [2, 512, 1024], replicated, may hold values from -0.25 to 0.25
- lstm_bias: float32 [2, 1024], replicated, may hold values from -4 to 4
Outputs:
- mixed: bfloat16 [16, 65536, 256], P('snap', 'vert')
All inputs are finite; a program needn't handle non-finite values.
Results may differ from a plain program's by a relative error of at most 0.007.
Values may be sent and summed in bfloat16 or wider, within the bound.
A program may use at most 128 MiB of HBM per device.

v0:
```python
import functools

import jax
import jax.numpy as jnp
from jax import lax
from jax.experimental import pallas as pl
from jax.experimental.pallas import tpu as pltpu
from jax.sharding import PartitionSpec as P

BS = 128
MESH = pl.DeviceIdType.MESH
UNROLL = 8
ORDER, COLUMN, KEEP, LAST = range(4)


def sigmoid(x):
    return 0.5 * jnp.tanh(0.5 * x) + 0.5


def whole_kernel(
    n, lists_hbm, rows_hbm, cols_hbm, features, vals, w1, w2, lstm_w, lstm_b, out,
    lists, rows, cols, ranks, table, feat0, feat1, tile0, tile1,
    ext0, ext1, ext2, ext3, pack0, pack1, pack2, pack3, running, conv, xbuf, hbuf, back0, back1, stage,
    weights1, weights2, weights, bias, h0, c0, h1, c1,
    load, store, tiny_sem, sort_sem, halo_send, halo_recv,
    send_even, send_odd, send_rest, recv_even, recv_odd, recv_rest, send_back, recv_back,
):
    me = lax.axis_index("snap")
    vert = lax.axis_index("vert")
    verts = lax.axis_size("vert")
    lower, higher = lax.rem(vert + verts - 1, verts), lax.rem(vert + 1, verts)
    blocks, width = conv.shape[1], conv.shape[-1]
    bound = lists.shape[0] // 2
    tiles = vals.shape[1]
    offsets = [4, 3, 5, 2, 6, 1, 7] if n == 8 else list(range(1, n))

    tiny = [
        pltpu.make_async_copy(a, b, tiny_sem.at[i])
        for i, (a, b) in enumerate(((lists_hbm, lists), (rows_hbm, rows), (cols_hbm, cols)))
    ]
    for copy in tiny:
        copy.start()
    sources = [w1, features.at[0], features.at[1], vals.at[0], vals.at[1], lstm_w, lstm_b, w2]
    targets = [weights1, feat0, feat1, tile0, tile1, weights, bias, weights2]
    loads = [pltpu.make_async_copy(a, b, load.at[i]) for i, (a, b) in enumerate(zip(sources, targets))]
    for copy in loads:
        copy.start()

    barrier = pltpu.get_barrier_semaphore()
    for d in range(1, n):
        pl.semaphore_signal(
            barrier, inc=1, device_id={"snap": lax.rem(me + d, n)}, device_id_type=MESH
        )
    for side in (lower, higher):
        pl.semaphore_signal(barrier, inc=1, device_id={"vert": side}, device_id_type=MESH)

    def project(block, weight):
        return jnp.dot(block, weight[...], preferred_element_type=jnp.float32).astype(jnp.bfloat16)

    def make_pack(source, weight, pack):
        for i in range(2 * bound):
            pack[i] = project(source[lists[i, vert]], weight)

    def halo_copies(pack, extended, index):
        down = pltpu.make_async_remote_copy(
            src_ref=pack.at[pl.ds(0, bound)],
            dst_ref=extended.at[pl.ds(bound + blocks, bound)],
            send_sem=halo_send.at[index, 0],
            recv_sem=halo_recv.at[index, 0],
            device_id={"vert": lower},
            device_id_type=MESH,
        )
        up = pltpu.make_async_remote_copy(
            src_ref=pack.at[pl.ds(bound, bound)],
            dst_ref=extended.at[pl.ds(0, bound)],
            send_sem=halo_send.at[index, 1],
            recv_sem=halo_recv.at[index, 1],
            device_id={"vert": higher},
            device_id_type=MESH,
        )
        return (down, up)

    def project_own(source, weight, extended):
        def some(g, carry):
            for u in range(4):
                i = 4 * g + u
                extended[bound + i] = project(source[i], weight)
            return carry

        lax.fori_loop(0, blocks // 4, some, 0)

    def convolve(s, extended, tile, finish):
        def group(g, carry):
            products = []
            for u in range(UNROLL):
                k = g * UNROLL + u
                products.append(
                    jnp.dot(
                        tile[table[4 * s + ORDER, k]],
                        extended[table[4 * s + COLUMN, k]],
                        preferred_element_type=jnp.float32,
                    )
                )
            total = running[g * UNROLL]
            for u in range(UNROLL):
                k = g * UNROLL + u
                total = total * table[4 * s + KEEP, k].astype(jnp.float32) + products[u]
                running[k + 1] = total
            return carry

        lax.fori_loop(0, tiles // UNROLL, group, 0)

        def row(g, carry):
            for u in range(4):
                r = 4 * g + u
                finish(r, running[table[4 * s + LAST, r]])
            return carry

        lax.fori_loop(0, blocks // 4, row, 0)

    def cross(source, slot, send, recv, peer):
        return pltpu.make_async_remote_copy(
            src_ref=source,
            dst_ref=slot,
            send_sem=send.at[peer],
            recv_sem=recv.at[me],
            device_id={"snap": peer},
            device_id_type=MESH,
        )

    def even_copy(peer):
        return cross(conv.at[0, 2 * peer], xbuf.at[0, 2 * me], send_even, recv_even, peer)

    def odd_copy(peer):
        return cross(conv.at[1, 2 * peer], xbuf.at[0, 2 * me + 1], send_odd, recv_odd, peer)

    def rest_copy(peer):
        return cross(
            conv.at[:, 2 * peer + 1], xbuf.at[1, pl.ds(2 * me, 2)], send_rest, recv_rest, peer
        )

    def landed(slot, semaphore):
        pltpu.make_async_copy(slot, slot, semaphore).wait()

    def sort_tiles():
        shape = (tiles, ranks.shape[1])
        lane = lax.broadcasted_iota(jnp.int32, shape, 1)
        sub = lax.broadcasted_iota(jnp.int32, shape, 0)
        square = (tiles, tiles)
        lane_sq = lax.broadcasted_iota(jnp.int32, square, 1)
        sub_sq = lax.broadcasted_iota(jnp.int32, square, 0)

        def upright(line):
            wide = jnp.broadcast_to(line, square)
            return jnp.sum(jnp.where(lane_sq == sub_sq, wide, 0), axis=1, keepdims=True)

        def pick(column, chosen):
            return jnp.sum(jnp.where(chosen, column, 0), axis=0, keepdims=True)

        for s in range(rows.shape[0]):
            row_line = rows[s : s + 1, :]
            row = upright(row_line)
            key_line = jnp.broadcast_to(row_line, square) * tiles + lane_sq
            smaller = jnp.where(key_line < row * tiles + sub_sq, 1, 0)
            rank = jnp.sum(smaller, axis=1, keepdims=True)
            chosen = rank == lane
            ranks[4 * s + ORDER : 4 * s + ORDER + 1, :] = pick(sub, chosen)
            ranks[4 * s + COLUMN : 4 * s + COLUMN + 1, :] = pick(upright(cols[s : s + 1, :]), chosen)
            line = pick(row, chosen)
            before = pltpu.roll(line, 1, axis=1)
            first = lax.broadcasted_iota(jnp.int32, line.shape, 1) == 0
            ranks[4 * s + KEEP : 4 * s + KEEP + 1, :] = jnp.where(
                first, 0, jnp.where(line == before, 1, 0)
            )
            upto = pick(jnp.ones_like(row), row <= lane)
            same = pick(jnp.ones_like(row), row == lane)
            ranks[4 * s + LAST : 4 * s + LAST + 1, :] = jnp.where(same > 0, upto, 0)
        return pltpu.make_async_copy(ranks, table, sort_sem)

    tiny[0].wait()
    running[0] = jnp.zeros_like(running[0])
    loads[0].wait()
    loads[1].wait()
    make_pack(feat0, weights1, pack0)
    pl.semaphore_wait(barrier, n + 1)
    halo0 = halo_copies(pack0, ext0, 0)
    for copy in halo0:
        copy.start()
    loads[2].wait()
    make_pack(feat1, weights1, pack1)
    halo1 = halo_copies(pack1, ext1, 1)
    for copy in halo1:
        copy.start()
    for copy in tiny[1:]:
        copy.wait()
    sorting = sort_tiles()
    sorting.start()
    project_own(feat0, weights1, ext0)
    project_own(feat1, weights1, ext1)

    def keep_conv(s):
        def finish(r, total):
            conv[s, r] = jnp.maximum(total, 0.0).astype(jnp.bfloat16)

        return finish

    sorting.wait()
    loads[3].wait()
    for copy in halo0:
        copy.wait_recv()
    convolve(0, ext0, tile0, keep_conv(0))
    for d in offsets:
        even_copy(lax.rem(me + d, n)).start()
    pltpu.make_async_copy(conv.at[0, 2 * me], xbuf.at[0, 2 * me], recv_even.at[me]).start()
    loads[4].wait()
    for copy in halo1:
        copy.wait_recv()
    convolve(1, ext1, tile1, keep_conv(1))
    for d in offsets:
        odd_copy(lax.rem(me + d, n)).start()
    pltpu.make_async_copy(conv.at[1, 2 * me], xbuf.at[0, 2 * me + 1], recv_odd.at[me]).start()
    for d in offsets:
        rest_copy(lax.rem(me + d, n)).start()
    pltpu.make_async_copy(
        conv.at[:, 2 * me + 1], xbuf.at[1, pl.ds(2 * me, 2)], recv_rest.at[me]
    ).start()

    for copy in loads[5:]:
        copy.wait()

    def cell(x, hidden, memory, layer):
        gates = (
            jnp.dot(x, weights[layer, :width], preferred_element_type=jnp.float32)
            + jnp.dot(hidden[...], weights[layer, width:], preferred_element_type=jnp.float32)
            + bias[layer][None, :]
        )
        kept = sigmoid(gates[:, width : 2 * width]) * memory[...]
        new = kept + sigmoid(gates[:, :width]) * jnp.tanh(gates[:, 2 * width : 3 * width])
        memory[...] = new
        result = (sigmoid(gates[:, 3 * width :]) * jnp.tanh(new)).astype(jnp.bfloat16)
        hidden[...] = result
        return result

    backs = (back0, back1)

    def back_copy(half, part, owner):
        return pltpu.make_async_remote_copy(
            src_ref=hbuf.at[half, 2 * owner + part],
            dst_ref=backs[part].at[2 * me + half],
            send_sem=send_back.at[half, part, owner],
            recv_sem=recv_back.at[half, part, me],
            device_id={"snap": owner},
            device_id_type=MESH,
        )

    def give_own(half, part):
        pltpu.make_async_copy(
            hbuf.at[half, 2 * me + part],
            backs[part].at[2 * me + half],
            recv_back.at[half, part, me],
        ).start()

    for half in range(2):
        h0[...] = jnp.zeros_like(h0)
        h1[...] = jnp.zeros_like(h1)
        c0[...] = jnp.zeros_like(c0)
        c1[...] = jnp.zeros_like(c1)

        def step(owner, carry, half=half):
            if half == 0:
                landed(xbuf.at[0, 2 * owner], recv_even.at[owner])
                landed(xbuf.at[0, 2 * owner + 1], recv_odd.at[owner])
            else:
                landed(xbuf.at[1, pl.ds(2 * owner, 2)], recv_rest.at[owner])
            for part in range(2):
                t = 2 * owner + part
                low = cell(xbuf[half, t], h0, c0, 0)
                hbuf[half, t] = cell(low, h1, c1, 1)
            return carry

        lax.fori_loop(0, n, step, 0)
        if half == 0:
            order = [(d, part) for d in offsets for part in range(2)]
        else:
            order = [(d, part) for part in range(2) for d in offsets]
        for d, part in order:
            back_copy(half, part, lax.rem(me + d, n)).start()
        for part in range(2):
            give_own(half, part)

    halos = []
    stores = []
    for part in range(2):
        back, pack, extended = backs[part], (pack2, pack3)[part], (ext2, ext3)[part]
        tile = (tile0, tile1)[part]

        def arrive(source, carry, part=part, back=back):
            for half in range(2):
                landed(back.at[2 * source + half], recv_back.at[half, part, source])
            return carry

        lax.fori_loop(0, n, arrive, 0)
        make_pack(back, weights2, pack)
        copies = halo_copies(pack, extended, 2 + part)
        for copy in copies:
            copy.start()
        project_own(back, weights2, extended)
        for copy in copies:
            copy.wait_recv()
        halos.append(copies)

        def finish(r, total, part=part):
            stage[part, r] = total.astype(jnp.bfloat16)

        convolve(part, extended, tile, finish)
        copy = pltpu.make_async_copy(stage.at[part], out.at[part], store.at[part])
        copy.start()
        stores.append(copy)

    def drain(i, carry):
        peer = lax.rem(me + i, n)
        even_copy(peer).wait_send()
        odd_copy(peer).wait_send()
        rest_copy(peer).wait_send()
        for half in range(2):
            for part in range(2):
                back_copy(half, part, peer).wait_send()
        return carry

    lax.fori_loop(1, n, drain, 0)
    for copies in [halo0, halo1] + halos:
        for copy in copies:
            copy.wait_send()
    for copy in stores:
        copy.wait()


def whole(send_lists, tile_rows, tile_cols, features, tile_vals, w1, w2, lstm_weight, lstm_bias):
    n = lax.axis_size("snap")
    snaps, blocks, _, width = features.shape
    bound = send_lists.shape[0] // 2
    tiles = tile_vals.shape[1]
    total = snaps * n
    hbm = pl.BlockSpec(memory_space=pltpu.HBM)

    def rows(count, dtype=jnp.bfloat16):
        return pltpu.VMEM((count, BS, width), dtype)

    def states(dtype):
        return pltpu.VMEM((BS, width), dtype)

    dma = pltpu.SemaphoreType.DMA
    operands = [
        pltpu.with_memory_space_constraint(x, pltpu.HBM)
        for x in (
            send_lists, tile_rows, tile_cols, features, tile_vals, w1, w2, lstm_weight, lstm_bias
        )
    ]
    return pl.pallas_call(
        functools.partial(whole_kernel, n),
        out_shape=jax.ShapeDtypeStruct(features.shape, jnp.bfloat16),
        in_specs=[hbm] * 9,
        out_specs=pl.BlockSpec(memory_space=pl.ANY),
        scratch_shapes=[
            pltpu.SMEM(send_lists.shape, jnp.int32), pltpu.VMEM(tile_rows.shape, jnp.int32),
            pltpu.VMEM(tile_cols.shape, jnp.int32),
            pltpu.VMEM((8, 128), jnp.int32), pltpu.SMEM((8, 128), jnp.int32),
            rows(blocks), rows(blocks),
            pltpu.VMEM((tiles, BS, BS), jnp.bfloat16), pltpu.VMEM((tiles, BS, BS), jnp.bfloat16),
            rows(blocks + 2 * bound), rows(blocks + 2 * bound),
            rows(blocks + 2 * bound), rows(blocks + 2 * bound),
            rows(2 * bound), rows(2 * bound), rows(2 * bound), rows(2 * bound),
            rows(tiles + 1, jnp.float32),
            pltpu.VMEM((snaps, blocks, BS, width), jnp.bfloat16),
            pltpu.VMEM((2, total, BS, width), jnp.bfloat16),
            pltpu.VMEM((2, total, BS, width), jnp.bfloat16),
            rows(blocks), rows(blocks),
            pltpu.VMEM((snaps, blocks, BS, width), jnp.bfloat16),
            pltpu.VMEM(w1.shape, jnp.bfloat16), pltpu.VMEM(w2.shape, jnp.bfloat16),
            pltpu.VMEM(lstm_weight.shape, jnp.bfloat16), pltpu.VMEM(lstm_bias.shape, jnp.float32),
            states(jnp.bfloat16), states(jnp.float32), states(jnp.bfloat16), states(jnp.float32),
            dma((8,)), dma((2,)), dma((3,)), dma(()), dma((4, 2)), dma((4, 2)),
            dma((n,)), dma((n,)), dma((n,)), dma((n,)), dma((n,)), dma((n,)),
            dma((2, 2, n)), dma((2, 2, n)),
        ],
        compiler_params=pltpu.CompilerParams(
            collective_id=0, has_side_effects=True, vmem_limit_bytes=44 * 2**20
        ),
        cost_estimate=pl.CostEstimate(
            flops=12 << 30, bytes_accessed=11 << 20, transcendentals=42 << 20
        ),
        name="whole",
    )(*operands)


def shards(
    features,
    tile_rows,
    tile_cols,
    tile_vals,
    send_lists,
    conv1_weight,
    conv2_weight,
    lstm_weight,
    lstm_bias,
):
    snapshots, vertices, width = features.shape
    own = features.reshape(snapshots, vertices // BS, BS, width)
    mixed = whole(
        send_lists.T, tile_rows, tile_cols, own, tile_vals,
        conv1_weight, conv2_weight, lstm_weight, lstm_bias,
    )
    return mixed.reshape(snapshots, vertices, width)


def solution(mesh):
    placed = (
        P("snap", "vert", None),
        P("snap", "vert"),
        P("snap", "vert"),
        P("snap", "vert", None, None),
        P(),
        P(),
        P(),
        P(),
        P(),
    )
    return jax.shard_map(
        shards, mesh=mesh, in_specs=placed, out_specs=P("snap", "vert", None), check_vma=False
    )
```

profile of v0, /device:TPU:64, one launch (start us, length us, event | category | flops | bytes accessed | tf_op | source)
XLA Modules:
  0.0 117.8 jit_solution(8780133220106208265)
XLA Ops:
  0.0 116.4 %whole.1 = bf16[2,16,128,256]{3,2,1,0:T(8,128)(2,1)S(1)} custom-call(s32[6,32]{1,0:T(8,128)} %bitcast.5, s32[2,64]{1,0:T(2,128)} %rows_hbm.1, s32[2,64]{1,0:T(2,128)} %cols_hbm.1, bf16[2,16,128,256]{3,2,1,0:T(8,128)(2,1)} %bitcast.4, bf16[2,64,128,128]{3,2,1,0:T(8,128)(2,1)} %vals.1, bf16[256,256]{1,0:T(8,128)(2,1)} %w1.1, bf16[256,256]{1,0:T(8,128)(2,1)} %w2.1, ...), custom_call_target="tpu_custom_call" | custom-call | flops 12884901888 | bytes 11534336 | tf_op jit(solution)/shard_map/whole/pallas_call | solution.py:359
  116.4 1.3 %copy.11 = bf16[2,2048,256]{2,1,0:T(8,128)(2,1)} copy(bf16[2,2048,256]{2,1,0:T(8,128)(2,1)S(1)} %bitcast.3) | data formatting | bytes 4194304
where the time goes:
time: 119 us; the launch traced here: 118 us
  Pallas kernels  116 us (97%)
  local copies, waits for them, and re-layouts  1.32 us (1%)
    pallas_call x1, Pallas kernels, whole(): pl.pallas_call(functools.partial(whole_kernel, n), out_shape=jax.ShapeDty...  116 us

commit v1 on v0

--- a/solution.py
+++ b/solution.py
@@ -9,8 +9,9 @@
 
 BS = 128
 MESH = pl.DeviceIdType.MESH
-UNROLL = 8
-ORDER, COLUMN, KEEP, LAST = range(4)
+UNROLL = 32
+ORDER, COLUMN, KEEP, LAST, AGAIN = range(5)
+BLOCK, PLACE = 10, 11
 
 
 def sigmoid(x):
@@ -20,9 +21,9 @@
 def whole_kernel(
     n, lists_hbm, rows_hbm, cols_hbm, features, vals, w1, w2, lstm_w, lstm_b, out,
     lists, rows, cols, ranks, table, feat0, feat1, tile0, tile1,
-    ext0, ext1, ext2, ext3, pack0, pack1, pack2, pack3, running, conv, xbuf, hbuf, back0, back1, stage,
+    ext0, ext1, ext2, ext3, pack0, pack1, pack2, pack3, running, conv, xbuf, hbuf, back0, back1, back2, back3,
     weights1, weights2, weights, bias, h0, c0, h1, c1,
-    load, store, tiny_sem, sort_sem, halo_send, halo_recv,
+    load, tiny_sem, sort_sem, halo_send, halo_recv,
     send_even, send_odd, send_rest, recv_even, recv_odd, recv_rest, send_back, recv_back,
 ):
     me = lax.axis_index("snap")
@@ -57,9 +58,9 @@
     def project(block, weight):
         return jnp.dot(block, weight[...], preferred_element_type=jnp.float32).astype(jnp.bfloat16)
 
-    def make_pack(source, weight, pack):
+    def make_pack(source, weight, pack, place):
         for i in range(2 * bound):
-            pack[i] = project(source[lists[i, vert]], weight)
+            pack[i] = project(source[place(lists[i, vert])], weight)
 
     def halo_copies(pack, extended, index):
         down = pltpu.make_async_remote_copy(
@@ -80,43 +81,43 @@
         )
         return (down, up)
 
-    def project_own(source, weight, extended):
+    def project_own(source, weight, extended, base):
         def some(g, carry):
             for u in range(4):
                 i = 4 * g + u
-                extended[bound + i] = project(source[i], weight)
+                extended[base + i] = project(source[i], weight)
             return carry
 
-        lax.fori_loop(0, blocks // 4, some, 0)
-
-    def convolve(s, extended, tile, finish):
+        lax.fori_loop(0, source.shape[0] // 4, some, 0)
+
+    def convolve(s, kind, extended, tile, block, finish):
         def group(g, carry):
             products = []
             for u in range(UNROLL):
                 k = g * UNROLL + u
                 products.append(
                     jnp.dot(
-                        tile[table[4 * s + ORDER, k]],
-                        extended[table[4 * s + COLUMN, k]],
+                        tile[table[2 * ORDER + s, k]],
+                        extended[table[2 * kind + s, k]],
                         preferred_element_type=jnp.float32,
                     )
                 )
             total = running[g * UNROLL]
             for u in range(UNROLL):
                 k = g * UNROLL + u
-                total = total * table[4 * s + KEEP, k].astype(jnp.float32) + products[u]
+                total = total * table[2 * KEEP + s, k].astype(jnp.float32) + products[u]
                 running[k + 1] = total
             return carry
 
         lax.fori_loop(0, tiles // UNROLL, group, 0)
 
-        def row(g, carry):
-            for u in range(4):
-                r = 4 * g + u
-                finish(r, running[table[4 * s + LAST, r]])
+        def some(g, carry):
+            for u in range(8):
+                r = 8 * g + u
+                finish(r, running[table[2 * LAST + s, block(r)]])
             return carry
 
-        lax.fori_loop(0, blocks // 4, row, 0)
+        lax.fori_loop(0, blocks // 8, some, 0)
 
     def cross(source, slot, send, recv, peer):
         return pltpu.make_async_remote_copy(
@@ -129,14 +130,14 @@
         )
 
     def even_copy(peer):
-        return cross(conv.at[0, 2 * peer], xbuf.at[0, 2 * me], send_even, recv_even, peer)
+        return cross(conv.at[0, peer], xbuf.at[0, 2 * me], send_even, recv_even, peer)
 
     def odd_copy(peer):
-        return cross(conv.at[1, 2 * peer], xbuf.at[0, 2 * me + 1], send_odd, recv_odd, peer)
+        return cross(conv.at[1, peer], xbuf.at[0, 2 * me + 1], send_odd, recv_odd, peer)
 
     def rest_copy(peer):
         return cross(
-            conv.at[:, 2 * peer + 1], xbuf.at[1, pl.ds(2 * me, 2)], send_rest, recv_rest, peer
+            conv.at[:, n + peer], xbuf.at[1, pl.ds(2 * me, 2)], send_rest, recv_rest, peer
         )
 
     def landed(slot, semaphore):
@@ -157,37 +158,67 @@
         def pick(column, chosen):
             return jnp.sum(jnp.where(chosen, column, 0), axis=0, keepdims=True)
 
+        few = (blocks, blocks)
+        lane_few = lax.broadcasted_iota(jnp.int32, few, 1)
+        sub_few = lax.broadcasted_iota(jnp.int32, few, 0)
+        lane_line = lax.broadcasted_iota(jnp.int32, (1, ranks.shape[1]), 1)
+
+        def line_at(kind, value):
+            ranks[kind : kind + 1, :] = value
+
+        def unlisted(index):
+            value = jnp.ones_like(index)
+            for i in range(2 * bound):
+                value = jnp.where(index == lists[i, vert], 0, value)
+            return value * blocks + index
+
+        key_up = unlisted(lax.broadcasted_iota(jnp.int32, (blocks, ranks.shape[1]), 0))
+        key_line = unlisted(lane_line)
+        place_line = jnp.sum(jnp.where(key_up < key_line, 1, 0), axis=0, keepdims=True)
+        line_at(PLACE, place_line)
+        smaller = jnp.where(unlisted(lane_few) < unlisted(sub_few), 1, 0)
+        place = jnp.sum(smaller, axis=1, keepdims=True)
+        wide = (blocks, ranks.shape[1])
+        line_at(
+            BLOCK,
+            pick(
+                lax.broadcasted_iota(jnp.int32, wide, 0),
+                place == lax.broadcasted_iota(jnp.int32, wide, 1),
+            ),
+        )
         for s in range(rows.shape[0]):
             row_line = rows[s : s + 1, :]
             row = upright(row_line)
-            key_line = jnp.broadcast_to(row_line, square) * tiles + lane_sq
-            smaller = jnp.where(key_line < row * tiles + sub_sq, 1, 0)
+            col = upright(cols[s : s + 1, :])
+            key = jnp.broadcast_to(row_line, square) * tiles + lane_sq
+            smaller = jnp.where(key < row * tiles + sub_sq, 1, 0)
             rank = jnp.sum(smaller, axis=1, keepdims=True)
             chosen = rank == lane
-            ranks[4 * s + ORDER : 4 * s + ORDER + 1, :] = pick(sub, chosen)
-            ranks[4 * s + COLUMN : 4 * s + COLUMN + 1, :] = pick(upright(cols[s : s + 1, :]), chosen)
+            line_at(2 * ORDER + s, pick(sub, chosen))
+            line_at(2 * COLUMN + s, pick(col, chosen))
+            moved = jnp.where(lane == col - bound, place_line, 0)
+            moved = jnp.sum(moved, axis=1, keepdims=True) + bound
+            inner = jnp.where(col >= bound, jnp.where(col < bound + blocks, 1, 0), 0)
+            line_at(2 * AGAIN + s, pick(jnp.where(inner == 1, moved, col), chosen))
             line = pick(row, chosen)
-            before = pltpu.roll(line, 1, axis=1)
-            first = lax.broadcasted_iota(jnp.int32, line.shape, 1) == 0
-            ranks[4 * s + KEEP : 4 * s + KEEP + 1, :] = jnp.where(
-                first, 0, jnp.where(line == before, 1, 0)
-            )
+            same = jnp.where(line == pltpu.roll(line, 1, axis=1), 1, 0)
+            line_at(2 * KEEP + s, jnp.where(lane_line == 0, 0, same))
             upto = pick(jnp.ones_like(row), row <= lane)
-            same = pick(jnp.ones_like(row), row == lane)
-            ranks[4 * s + LAST : 4 * s + LAST + 1, :] = jnp.where(same > 0, upto, 0)
+            found = pick(jnp.ones_like(row), row == lane)
+            line_at(2 * LAST + s, jnp.where(found > 0, upto, 0))
         return pltpu.make_async_copy(ranks, table, sort_sem)
 
     tiny[0].wait()
     running[0] = jnp.zeros_like(running[0])
     loads[0].wait()
     loads[1].wait()
-    make_pack(feat0, weights1, pack0)
+    make_pack(feat0, weights1, pack0, lambda b: b)
     pl.semaphore_wait(barrier, n + 1)
     halo0 = halo_copies(pack0, ext0, 0)
     for copy in halo0:
         copy.start()
     loads[2].wait()
-    make_pack(feat1, weights1, pack1)
+    make_pack(feat1, weights1, pack1, lambda b: b)
     halo1 = halo_copies(pack1, ext1, 1)
     for copy in halo1:
         copy.start()
@@ -195,8 +226,8 @@
         copy.wait()
     sorting = sort_tiles()
     sorting.start()
-    project_own(feat0, weights1, ext0)
-    project_own(feat1, weights1, ext1)
+    project_own(feat0, weights1, ext0, bound)
+    project_own(feat1, weights1, ext1, bound)
 
     def keep_conv(s):
         def finish(r, total):
@@ -208,21 +239,21 @@
     loads[3].wait()
     for copy in halo0:
         copy.wait_recv()
-    convolve(0, ext0, tile0, keep_conv(0))
+    convolve(0, COLUMN, ext0, tile0, lambda p: table[BLOCK, p], keep_conv(0))
     for d in offsets:
         even_copy(lax.rem(me + d, n)).start()
-    pltpu.make_async_copy(conv.at[0, 2 * me], xbuf.at[0, 2 * me], recv_even.at[me]).start()
+    pltpu.make_async_copy(conv.at[0, me], xbuf.at[0, 2 * me], recv_even.at[me]).start()
     loads[4].wait()
     for copy in halo1:
         copy.wait_recv()
-    convolve(1, ext1, tile1, keep_conv(1))
+    convolve(1, COLUMN, ext1, tile1, lambda p: table[BLOCK, p], keep_conv(1))
     for d in offsets:
         odd_copy(lax.rem(me + d, n)).start()
-    pltpu.make_async_copy(conv.at[1, 2 * me], xbuf.at[0, 2 * me + 1], recv_odd.at[me]).start()
+    pltpu.make_async_copy(conv.at[1, me], xbuf.at[0, 2 * me + 1], recv_odd.at[me]).start()
     for d in offsets:
         rest_copy(lax.rem(me + d, n)).start()
     pltpu.make_async_copy(
-        conv.at[:, 2 * me + 1], xbuf.at[1, pl.ds(2 * me, 2)], recv_rest.at[me]
+        conv.at[:, n + me], xbuf.at[1, pl.ds(2 * me, 2)], recv_rest.at[me]
     ).start()
 
     for copy in loads[5:]:
@@ -241,12 +272,12 @@
         hidden[...] = result
         return result
 
-    backs = (back0, back1)
+    backs = ((back0, back1), (back2, back3))
 
     def back_copy(half, part, owner):
         return pltpu.make_async_remote_copy(
             src_ref=hbuf.at[half, 2 * owner + part],
-            dst_ref=backs[part].at[2 * me + half],
+            dst_ref=backs[part][half].at[me],
             send_sem=send_back.at[half, part, owner],
             recv_sem=recv_back.at[half, part, me],
             device_id={"snap": owner},
@@ -256,7 +287,7 @@
     def give_own(half, part):
         pltpu.make_async_copy(
             hbuf.at[half, 2 * me + part],
-            backs[part].at[2 * me + half],
+            backs[part][half].at[me],
             recv_back.at[half, part, me],
         ).start()
 
@@ -288,34 +319,34 @@
         for part in range(2):
             give_own(half, part)
 
+    def arrive(part, half):
+        def one(source, carry):
+            landed(backs[part][half].at[source], recv_back.at[half, part, source])
+            return carry
+
+        lax.fori_loop(0, n, one, 0)
+
+    packs, wides, grids = (pack2, pack3), (ext2, ext3), (tile0, tile1)
     halos = []
-    stores = []
     for part in range(2):
-        back, pack, extended = backs[part], (pack2, pack3)[part], (ext2, ext3)[part]
-        tile = (tile0, tile1)[part]
-
-        def arrive(source, carry, part=part, back=back):
-            for half in range(2):
-                landed(back.at[2 * source + half], recv_back.at[half, part, source])
-            return carry
-
-        lax.fori_loop(0, n, arrive, 0)
-        make_pack(back, weights2, pack)
-        copies = halo_copies(pack, extended, 2 + part)
+        arrive(part, 0)
+        make_pack(backs[part][0], weights2, packs[part], lambda b: table[PLACE, b])
+        copies = halo_copies(packs[part], wides[part], 2 + part)
         for copy in copies:
             copy.start()
-        project_own(back, weights2, extended)
-        for copy in copies:
+        halos.append(copies)
+    for part in range(2):
+        project_own(backs[part][0], weights2, wides[part], bound)
+    for part in range(2):
+        arrive(part, 1)
+        project_own(backs[part][1], weights2, wides[part], bound + n)
+        for copy in halos[part]:
             copy.wait_recv()
-        halos.append(copies)
 
         def finish(r, total, part=part):
-            stage[part, r] = total.astype(jnp.bfloat16)
-
-        convolve(part, extended, tile, finish)
-        copy = pltpu.make_async_copy(stage.at[part], out.at[part], store.at[part])
-        copy.start()
-        stores.append(copy)
+            out[part, r] = total.astype(jnp.bfloat16)
+
+        convolve(part, AGAIN, wides[part], grids[part], lambda r: r, finish)
 
     def drain(i, carry):
         peer = lax.rem(me + i, n)
@@ -331,8 +362,6 @@
     for copies in [halo0, halo1] + halos:
         for copy in copies:
             copy.wait_send()
-    for copy in stores:
-        copy.wait()
 
 
 def whole(send_lists, tile_rows, tile_cols, features, tile_vals, w1, w2, lstm_weight, lstm_bias):
@@ -360,11 +389,11 @@
         functools.partial(whole_kernel, n),
         out_shape=jax.ShapeDtypeStruct(features.shape, jnp.bfloat16),
         in_specs=[hbm] * 9,
-        out_specs=pl.BlockSpec(memory_space=pl.ANY),
+        out_specs=pl.BlockSpec(memory_space=pltpu.VMEM),
         scratch_shapes=[
             pltpu.SMEM(send_lists.shape, jnp.int32), pltpu.VMEM(tile_rows.shape, jnp.int32),
             pltpu.VMEM(tile_cols.shape, jnp.int32),
-            pltpu.VMEM((8, 128), jnp.int32), pltpu.SMEM((8, 128), jnp.int32),
+            pltpu.VMEM((16, 128), jnp.int32), pltpu.SMEM((16, 128), jnp.int32),
             rows(blocks), rows(blocks),
             pltpu.VMEM((tiles, BS, BS), jnp.bfloat16), pltpu.VMEM((tiles, BS, BS), jnp.bfloat16),
             rows(blocks + 2 * bound), rows(blocks + 2 * bound),
@@ -374,12 +403,11 @@
             pltpu.VMEM((snaps, blocks, BS, width), jnp.bfloat16),
             pltpu.VMEM((2, total, BS, width), jnp.bfloat16),
             pltpu.VMEM((2, total, BS, width), jnp.bfloat16),
-            rows(blocks), rows(blocks),
-            pltpu.VMEM((snaps, blocks, BS, width), jnp.bfloat16),
+            rows(n), rows(n), rows(n), rows(n),
             pltpu.VMEM(w1.shape, jnp.bfloat16), pltpu.VMEM(w2.shape, jnp.bfloat16),
             pltpu.VMEM(lstm_weight.shape, jnp.bfloat16), pltpu.VMEM(lstm_bias.shape, jnp.float32),
             states(jnp.bfloat16), states(jnp.float32), states(jnp.bfloat16), states(jnp.float32),
-            dma((8,)), dma((2,)), dma((3,)), dma(()), dma((4, 2)), dma((4, 2)),
+            dma((8,)), dma((3,)), dma(()), dma((4, 2)), dma((4, 2)),
             dma((n,)), dma((n,)), dma((n,)), dma((n,)), dma((n,)), dma((n,)),
             dma((2, 2, n)), dma((2, 2, n)),
         ],

time: 119 us -> 111 us (0.933); the launches traced: 118 us -> 109 us
  Pallas kernels: 116 us -> 107 us
    pallas_call x1, Pallas kernels: 116 us -> 107 us  [whole(): pl.pallas_call(functools.partial(whole_kernel, n), out_shape=jax.ShapeDty...]
where the time goes in v1:
time: 111 us; the launch traced here: 109 us
  Pallas kernels  107 us (96%)
  local copies, waits for them, and re-layouts  1.32 us (1%)
    pallas_call x1, Pallas kernels, whole(): pl.pallas_call(functools.partial(whole_kernel, n), out_shape=jax.ShapeDty...  107 us

profile of v1, /device:TPU:64, one launch (start us, length us, event | category | flops | bytes accessed | tf_op | source)
XLA Modules:
  0.0 108.6 jit_solution(13765482750460962286)
XLA Ops:
  0.0 107.2 %whole.1 = bf16[2,16,128,256]{3,2,1,0:T(8,128)(2,1)S(1)} custom-call(s32[6,32]{1,0:T(8,128)} %bitcast.5, s32[2,64]{1,0:T(2,128)} %rows_hbm.1, s32[2,64]{1,0:T(2,128)} %cols_hbm.1, bf16[2,16,128,256]{3,2,1,0:T(8,128)(2,1)} %bitcast.4, bf16[2,64,128,128]{3,2,1,0:T(8,128)(2,1)} %vals.1, bf16[256,256]{1,0:T(8,128)(2,1)} %w1.1, bf16[256,256]{1,0:T(8,128)(2,1)} %w2.1, ...), custom_call_target="tpu_custom_call" | custom-call | flops 12884901888 | bytes 11534336 | tf_op jit(solution)/shard_map/whole/pallas_call | solution.py:388
  107.2 1.3 %copy.11 = bf16[2,2048,256]{2,1,0:T(8,128)(2,1)} copy(bf16[2,2048,256]{2,1,0:T(8,128)(2,1)S(1)} %bitcast.3) | data formatting | bytes 4194304

commit v2 on v1

--- a/solution.py
+++ b/solution.py
@@ -9,9 +9,9 @@
 
 BS = 128
 MESH = pl.DeviceIdType.MESH
-UNROLL = 32
-ORDER, COLUMN, KEEP, LAST, AGAIN = range(5)
-BLOCK, PLACE = 10, 11
+UNROLL = 20
+KEEP, LAST, ORDER, COLUMN, AGAIN = 0, 1, 2, 4, 6
+BLOCK, PLACE = 16, 17
 
 
 def sigmoid(x):
@@ -33,27 +33,28 @@
     blocks, width = conv.shape[1], conv.shape[-1]
     bound = lists.shape[0] // 2
     tiles = vals.shape[1]
+    pairs = (tiles + blocks) // 2
     offsets = [4, 3, 5, 2, 6, 1, 7] if n == 8 else list(range(1, n))
 
     tiny = [
         pltpu.make_async_copy(a, b, tiny_sem.at[i])
         for i, (a, b) in enumerate(((lists_hbm, lists), (rows_hbm, rows), (cols_hbm, cols)))
     ]
-    for copy in tiny:
-        copy.start()
     sources = [w1, features.at[0], features.at[1], vals.at[0], vals.at[1], lstm_w, lstm_b, w2]
-    targets = [weights1, feat0, feat1, tile0, tile1, weights, bias, weights2]
+    targets = [
+        weights1, feat0, feat1, tile0.at[pl.ds(0, tiles)], tile1.at[pl.ds(0, tiles)],
+        weights, bias, weights2,
+    ]
     loads = [pltpu.make_async_copy(a, b, load.at[i]) for i, (a, b) in enumerate(zip(sources, targets))]
-    for copy in loads:
-        copy.start()
-
     barrier = pltpu.get_barrier_semaphore()
+    for side in (lower, higher):
+        pl.semaphore_signal(barrier, inc=1, device_id={"vert": side}, device_id_type=MESH)
     for d in range(1, n):
         pl.semaphore_signal(
             barrier, inc=1, device_id={"snap": lax.rem(me + d, n)}, device_id_type=MESH
         )
-    for side in (lower, higher):
-        pl.semaphore_signal(barrier, inc=1, device_id={"vert": side}, device_id_type=MESH)
+    for copy in [tiny[0]] + loads[:2]:
+        copy.start()
 
     def project(block, weight):
         return jnp.dot(block, weight[...], preferred_element_type=jnp.float32).astype(jnp.bfloat16)
@@ -90,34 +91,34 @@
 
         lax.fori_loop(0, source.shape[0] // 4, some, 0)
 
-    def convolve(s, kind, extended, tile, block, finish):
+    def convolve(s, kind, extended, tile, block, finish, between=None):
         def group(g, carry):
             products = []
             for u in range(UNROLL):
-                k = g * UNROLL + u
+                q = g * UNROLL + u
+                left = [tile[table[2 * (ORDER + side) + s, q]] for side in range(2)]
+                right = [extended[table[2 * (kind + side) + s, q]] for side in range(2)]
                 products.append(
                     jnp.dot(
-                        tile[table[2 * ORDER + s, k]],
-                        extended[table[2 * kind + s, k]],
+                        jnp.concatenate(left, axis=1),
+                        jnp.concatenate(right, axis=0),
                         preferred_element_type=jnp.float32,
                     )
                 )
             total = running[g * UNROLL]
             for u in range(UNROLL):
-                k = g * UNROLL + u
-                total = total * table[2 * KEEP + s, k].astype(jnp.float32) + products[u]
-                running[k + 1] = total
+                q = g * UNROLL + u
+                total = total * table[2 * KEEP + s, q].astype(jnp.float32) + products[u]
+                running[q + 1] = total
             return carry
 
-        lax.fori_loop(0, tiles // UNROLL, group, 0)
-
-        def some(g, carry):
-            for u in range(8):
-                r = 8 * g + u
+        lax.fori_loop(0, pairs // UNROLL, group, 0)
+        for half in range(2):
+            for u in range(n):
+                r = half * n + u
                 finish(r, running[table[2 * LAST + s, block(r)]])
-            return carry
-
-        lax.fori_loop(0, blocks // 8, some, 0)
+            if between is not None and half == 0:
+                between()
 
     def cross(source, slot, send, recv, peer):
         return pltpu.make_async_remote_copy(
@@ -190,28 +191,42 @@
             row_line = rows[s : s + 1, :]
             row = upright(row_line)
             col = upright(cols[s : s + 1, :])
-            key = jnp.broadcast_to(row_line, square) * tiles + lane_sq
-            smaller = jnp.where(key < row * tiles + sub_sq, 1, 0)
-            rank = jnp.sum(smaller, axis=1, keepdims=True)
-            chosen = rank == lane
-            line_at(2 * ORDER + s, pick(sub, chosen))
-            line_at(2 * COLUMN + s, pick(col, chosen))
+            earlier = jnp.where(lane_sq < sub_sq, 1, 0)
+            alike = jnp.where(jnp.broadcast_to(row_line, square) == row, earlier, 0)
+            within = jnp.sum(alike, axis=1, keepdims=True)
+            found = pick(jnp.ones_like(row), row == lane)
+            padded = found + (found & 1)
+            base = jnp.sum(jnp.where(lane < row, padded, 0), axis=1, keepdims=True)
+            spot = base + within
             moved = jnp.where(lane == col - bound, place_line, 0)
             moved = jnp.sum(moved, axis=1, keepdims=True) + bound
             inner = jnp.where(col >= bound, jnp.where(col < bound + blocks, 1, 0), 0)
-            line_at(2 * AGAIN + s, pick(jnp.where(inner == 1, moved, col), chosen))
-            line = pick(row, chosen)
+            again = jnp.where(inner == 1, moved, col)
+            for side in range(2):
+                chosen = spot == 2 * lane + side
+                count = pick(jnp.ones_like(row), chosen)
+                line_at(2 * (ORDER + side) + s, jnp.where(count > 0, pick(sub, chosen), tiles))
+                line_at(2 * (COLUMN + side) + s, pick(col, chosen))
+                line_at(2 * (AGAIN + side) + s, pick(again, chosen))
+            line = pick(row, spot == 2 * lane)
             same = jnp.where(line == pltpu.roll(line, 1, axis=1), 1, 0)
             line_at(2 * KEEP + s, jnp.where(lane_line == 0, 0, same))
-            upto = pick(jnp.ones_like(row), row <= lane)
-            found = pick(jnp.ones_like(row), row == lane)
-            line_at(2 * LAST + s, jnp.where(found > 0, upto, 0))
+            wide_pad = jnp.broadcast_to(padded, wide)
+            wide_lane = lax.broadcasted_iota(jnp.int32, wide, 1)
+            wide_sub = lax.broadcasted_iota(jnp.int32, wide, 0)
+            pad = jnp.sum(jnp.where(wide_lane == wide_sub, wide_pad, 0), axis=1, keepdims=True)
+            upto = jnp.sum(jnp.where(wide_sub <= wide_lane, pad, 0), axis=0, keepdims=True)
+            line_at(2 * LAST + s, jnp.where(found > 0, upto >> 1, 0))
         return pltpu.make_async_copy(ranks, table, sort_sem)
 
     tiny[0].wait()
     running[0] = jnp.zeros_like(running[0])
+    for tile in (tile0, tile1):
+        tile[tiles] = jnp.zeros_like(tile[tiles])
     loads[0].wait()
     loads[1].wait()
+    for copy in loads[2:] + tiny[1:]:
+        copy.start()
     make_pack(feat0, weights1, pack0, lambda b: b)
     pl.semaphore_wait(barrier, n + 1)
     halo0 = halo_copies(pack0, ext0, 0)
@@ -239,10 +254,13 @@
     loads[3].wait()
     for copy in halo0:
         copy.wait_recv()
-    convolve(0, COLUMN, ext0, tile0, lambda p: table[BLOCK, p], keep_conv(0))
-    for d in offsets:
-        even_copy(lax.rem(me + d, n)).start()
-    pltpu.make_async_copy(conv.at[0, me], xbuf.at[0, 2 * me], recv_even.at[me]).start()
+
+    def send_evens():
+        for d in offsets:
+            even_copy(lax.rem(me + d, n)).start()
+        pltpu.make_async_copy(conv.at[0, me], xbuf.at[0, 2 * me], recv_even.at[me]).start()
+
+    convolve(0, COLUMN, ext0, tile0, lambda p: table[BLOCK, p], keep_conv(0), send_evens)
     loads[4].wait()
     for copy in halo1:
         copy.wait_recv()
@@ -393,13 +411,14 @@
         scratch_shapes=[
             pltpu.SMEM(send_lists.shape, jnp.int32), pltpu.VMEM(tile_rows.shape, jnp.int32),
             pltpu.VMEM(tile_cols.shape, jnp.int32),
-            pltpu.VMEM((16, 128), jnp.int32), pltpu.SMEM((16, 128), jnp.int32),
+            pltpu.VMEM((24, 128), jnp.int32), pltpu.SMEM((24, 128), jnp.int32),
             rows(blocks), rows(blocks),
-            pltpu.VMEM((tiles, BS, BS), jnp.bfloat16), pltpu.VMEM((tiles, BS, BS), jnp.bfloat16),
+            pltpu.VMEM((tiles + 1, BS, BS), jnp.bfloat16),
+            pltpu.VMEM((tiles + 1, BS, BS), jnp.bfloat16),
             rows(blocks + 2 * bound), rows(blocks + 2 * bound),
             rows(blocks + 2 * bound), rows(blocks + 2 * bound),
             rows(2 * bound), rows(2 * bound), rows(2 * bound), rows(2 * bound),
-            rows(tiles + 1, jnp.float32),
+            rows((tiles + blocks) // 2 + 1, jnp.float32),
             pltpu.VMEM((snaps, blocks, BS, width), jnp.bfloat16),
             pltpu.VMEM((2, total, BS, width), jnp.bfloat16),
             pltpu.VMEM((2, total, BS, width), jnp.bfloat16),

time: 111 us -> 110 us (level)
  no operation moved by 1% of the time
where the time goes in v2:
time: 110 us; the launch traced here: 108 us
  Pallas kernels  107 us (97%)
  local copies, waits for them, and re-layouts  1.32 us (1%)
    pallas_call x1, Pallas kernels, whole(): pl.pallas_call(functools.partial(whole_kernel, n), out_shape=jax.ShapeDty...  107 us

profile of v2, /device:TPU:64, one launch (start us, length us, event | category | flops | bytes accessed | tf_op | source)
XLA Modules:
  0.0 107.8 jit_solution(10282929402665022833)
XLA Ops:
  0.0 106.5 %whole.1 = bf16[2,16,128,256]{3,2,1,0:T(8,128)(2,1)S(1)} custom-call(s32[6,32]{1,0:T(8,128)} %bitcast.5, s32[2,64]{1,0:T(2,128)} %rows_hbm.1, s32[2,64]{1,0:T(2,128)} %cols_hbm.1, bf16[2,16,128,256]{3,2,1,0:T(8,128)(2,1)} %bitcast.4, bf16[2,64,128,128]{3,2,1,0:T(8,128)(2,1)} %vals.1, bf16[256,256]{1,0:T(8,128)(2,1)} %w1.1, bf16[256,256]{1,0:T(8,128)(2,1)} %w2.1, ...), custom_call_target="tpu_custom_call" | custom-call | flops 12884901888 | bytes 11534336 | tf_op jit(solution)/shard_map/whole/pallas_call | solution.py:406
  106.5 1.3 %copy.11 = bf16[2,2048,256]{2,1,0:T(8,128)(2,1)} copy(bf16[2,2048,256]{2,1,0:T(8,128)(2,1)S(1)} %bitcast.3) | data formatting | bytes 4194304

commit v3 on v2

--- a/solution.py
+++ b/solution.py
@@ -21,10 +21,10 @@
 def whole_kernel(
     n, lists_hbm, rows_hbm, cols_hbm, features, vals, w1, w2, lstm_w, lstm_b, out,
     lists, rows, cols, ranks, table, feat0, feat1, tile0, tile1,
-    ext0, ext1, ext2, ext3, pack0, pack1, pack2, pack3, running, conv, xbuf, hbuf, back0, back1, back2, back3,
+    ext0, ext1, ext2, ext3, pack0, pack1, pack2, pack3, running, conv, xbuf, hbuf, early, late0, late1,
     weights1, weights2, weights, bias, h0, c0, h1, c1,
     load, tiny_sem, sort_sem, halo_send, halo_recv,
-    send_even, send_odd, send_rest, recv_even, recv_odd, recv_rest, send_back, recv_back,
+    send_even, send_odd, send_rest, recv_even, recv_odd, recv_rest, send_early, recv_early, send_late, recv_late,
 ):
     me = lax.axis_index("snap")
     vert = lax.axis_index("vert")
@@ -59,9 +59,9 @@
     def project(block, weight):
         return jnp.dot(block, weight[...], preferred_element_type=jnp.float32).astype(jnp.bfloat16)
 
-    def make_pack(source, weight, pack, place):
+    def make_pack(source, weight, pack):
         for i in range(2 * bound):
-            pack[i] = project(source[place(lists[i, vert])], weight)
+            pack[i] = project(source(lists[i, vert]), weight)
 
     def halo_copies(pack, extended, index):
         down = pltpu.make_async_remote_copy(
@@ -82,14 +82,14 @@
         )
         return (down, up)
 
-    def project_own(source, weight, extended, base):
+    def project_own(source, count, weight, extended, base):
         def some(g, carry):
             for u in range(4):
                 i = 4 * g + u
-                extended[base + i] = project(source[i], weight)
+                extended[base + i] = project(source(i), weight)
             return carry
 
-        lax.fori_loop(0, source.shape[0] // 4, some, 0)
+        lax.fori_loop(0, count // 4, some, 0)
 
     def convolve(s, kind, extended, tile, block, finish, between=None):
         def group(g, carry):
@@ -227,13 +227,13 @@
     loads[1].wait()
     for copy in loads[2:] + tiny[1:]:
         copy.start()
-    make_pack(feat0, weights1, pack0, lambda b: b)
+    make_pack(lambda b: feat0[b], weights1, pack0)
     pl.semaphore_wait(barrier, n + 1)
     halo0 = halo_copies(pack0, ext0, 0)
     for copy in halo0:
         copy.start()
     loads[2].wait()
-    make_pack(feat1, weights1, pack1, lambda b: b)
+    make_pack(lambda b: feat1[b], weights1, pack1)
     halo1 = halo_copies(pack1, ext1, 1)
     for copy in halo1:
         copy.start()
@@ -241,8 +241,7 @@
         copy.wait()
     sorting = sort_tiles()
     sorting.start()
-    project_own(feat0, weights1, ext0, bound)
-    project_own(feat1, weights1, ext1, bound)
+    project_own(lambda i: feat0[i], blocks, weights1, ext0, bound)
 
     def keep_conv(s):
         def finish(r, total):
@@ -261,6 +260,7 @@
         pltpu.make_async_copy(conv.at[0, me], xbuf.at[0, 2 * me], recv_even.at[me]).start()
 
     convolve(0, COLUMN, ext0, tile0, lambda p: table[BLOCK, p], keep_conv(0), send_evens)
+    project_own(lambda i: feat1[i], blocks, weights1, ext1, bound)
     loads[4].wait()
     for copy in halo1:
         copy.wait_recv()
@@ -290,24 +290,18 @@
         hidden[...] = result
         return result
 
-    backs = ((back0, back1), (back2, back3))
-
-    def back_copy(half, part, owner):
-        return pltpu.make_async_remote_copy(
-            src_ref=hbuf.at[half, 2 * owner + part],
-            dst_ref=backs[part][half].at[me],
-            send_sem=send_back.at[half, part, owner],
-            recv_sem=recv_back.at[half, part, me],
-            device_id={"snap": owner},
-            device_id_type=MESH,
-        )
-
-    def give_own(half, part):
-        pltpu.make_async_copy(
-            hbuf.at[half, 2 * me + part],
-            backs[part][half].at[me],
-            recv_back.at[half, part, me],
-        ).start()
+    lates = (late0, late1)
+
+    def early_copy(owner):
+        return cross(
+            hbuf.at[0, pl.ds(2 * owner, 2)], early.at[me], send_early, recv_early, owner
+        )
+
+    def late_copy(part, owner):
+        return cross(
+            hbuf.at[1, 2 * owner + part], lates[part].at[me],
+            send_late.at[part], recv_late.at[part], owner,
+        )
 
     for half in range(2):
         h0[...] = jnp.zeros_like(h0)
@@ -329,57 +323,71 @@
 
         lax.fori_loop(0, n, step, 0)
         if half == 0:
-            order = [(d, part) for d in offsets for part in range(2)]
+            for d in offsets:
+                early_copy(lax.rem(me + d, n)).start()
+            pltpu.make_async_copy(
+                hbuf.at[0, pl.ds(2 * me, 2)], early.at[me], recv_early.at[me]
+            ).start()
         else:
-            order = [(d, part) for part in range(2) for d in offsets]
-        for d, part in order:
-            back_copy(half, part, lax.rem(me + d, n)).start()
-        for part in range(2):
-            give_own(half, part)
-
-    def arrive(part, half):
+            for part in range(2):
+                for d in offsets:
+                    late_copy(part, lax.rem(me + d, n)).start()
+                pltpu.make_async_copy(
+                    hbuf.at[1, 2 * me + part], lates[part].at[me], recv_late.at[part, me]
+                ).start()
+
+    def arrive(slots, semaphore):
         def one(source, carry):
-            landed(backs[part][half].at[source], recv_back.at[half, part, source])
+            landed(slots.at[source], semaphore.at[source])
             return carry
 
         lax.fori_loop(0, n, one, 0)
+
+    def drain(i, carry):
+        peer = lax.rem(me + i, n)
+        even_copy(peer).wait_send()
+        odd_copy(peer).wait_send()
+        rest_copy(peer).wait_send()
+        early_copy(peer).wait_send()
+        late_copy(0, peer).wait_send()
+        return carry
 
     packs, wides, grids = (pack2, pack3), (ext2, ext3), (tile0, tile1)
     halos = []
+    arrive(early, recv_early)
     for part in range(2):
-        arrive(part, 0)
-        make_pack(backs[part][0], weights2, packs[part], lambda b: table[PLACE, b])
+        make_pack(
+            lambda b, part=part: early[table[PLACE, b], part], weights2, packs[part]
+        )
         copies = halo_copies(packs[part], wides[part], 2 + part)
         for copy in copies:
             copy.start()
         halos.append(copies)
     for part in range(2):
-        project_own(backs[part][0], weights2, wides[part], bound)
+        project_own(lambda i, part=part: early[i, part], n, weights2, wides[part], bound)
     for part in range(2):
-        arrive(part, 1)
-        project_own(backs[part][1], weights2, wides[part], bound + n)
+        if part == 1:
+            lax.fori_loop(1, n, drain, 0)
+            for copies in [halo0, halo1] + halos:
+                for copy in copies:
+                    copy.wait_send()
         for copy in halos[part]:
             copy.wait_recv()
+        arrive(lates[part], recv_late.at[part])
+        project_own(
+            lambda i, part=part: lates[part][i], n, weights2, wides[part], bound + n
+        )
 
         def finish(r, total, part=part):
             out[part, r] = total.astype(jnp.bfloat16)
 
         convolve(part, AGAIN, wides[part], grids[part], lambda r: r, finish)
 
-    def drain(i, carry):
-        peer = lax.rem(me + i, n)
-        even_copy(peer).wait_send()
-        odd_copy(peer).wait_send()
-        rest_copy(peer).wait_send()
-        for half in range(2):
-            for part in range(2):
-                back_copy(half, part, peer).wait_send()
+    def last(i, carry):
+        late_copy(1, lax.rem(me + i, n)).wait_send()
         return carry
 
-    lax.fori_loop(1, n, drain, 0)
-    for copies in [halo0, halo1] + halos:
-        for copy in copies:
-            copy.wait_send()
+    lax.fori_loop(1, n, last, 0)
 
 
 def whole(send_lists, tile_rows, tile_cols, features, tile_vals, w1, w2, lstm_weight, lstm_bias):
@@ -422,13 +430,13 @@
             pltpu.VMEM((snaps, blocks, BS, width), jnp.bfloat16),
             pltpu.VMEM((2, total, BS, width), jnp.bfloat16),
             pltpu.VMEM((2, total, BS, width), jnp.bfloat16),
-            rows(n), rows(n), rows(n), rows(n),
+            pltpu.VMEM((n, 2, BS, width), jnp.bfloat16), rows(n), rows(n),
             pltpu.VMEM(w1.shape, jnp.bfloat16), pltpu.VMEM(w2.shape, jnp.bfloat16),
             pltpu.VMEM(lstm_weight.shape, jnp.bfloat16), pltpu.VMEM(lstm_bias.shape, jnp.float32),
             states(jnp.bfloat16), states(jnp.float32), states(jnp.bfloat16), states(jnp.float32),
             dma((8,)), dma((3,)), dma(()), dma((4, 2)), dma((4, 2)),
             dma((n,)), dma((n,)), dma((n,)), dma((n,)), dma((n,)), dma((n,)),
-            dma((2, 2, n)), dma((2, 2, n)),
+            dma((n,)), dma((n,)), dma((2, n)), dma((2, n)),
         ],
         compiler_params=pltpu.CompilerParams(
             collective_id=0, has_side_effects=True, vmem_limit_bytes=44 * 2**20

time: 110 us -> 110 us (level)
  the two profiles are of different devices: /device:TPU:64 before, /device:TPU:4 now
where the time goes in v3:
time: 110 us
  Pallas kernels  108 us (98%)
  local copies, waits for them, and re-layouts  1.32 us (1%)
    pallas_call x1, Pallas kernels, whole(): pl.pallas_call(functools.partial(whole_kernel, n), out_shape=jax.ShapeDty...  108 us

profile of v3, /device:TPU:4, one launch (start us, length us, event | category | flops | bytes accessed | tf_op | source)
XLA Modules:
  0.0 109.7 jit_solution(11194719496715201132)
XLA Ops:
  0.0 108.4 %whole.1 = bf16[2,16,128,256]{3,2,1,0:T(8,128)(2,1)S(1)} custom-call(s32[6,32]{1,0:T(8,128)} %bitcast.5, s32[2,64]{1,0:T(2,128)} %rows_hbm.1, s32[2,64]{1,0:T(2,128)} %cols_hbm.1, bf16[2,16,128,256]{3,2,1,0:T(8,128)(2,1)} %bitcast.4, bf16[2,64,128,128]{3,2,1,0:T(8,128)(2,1)} %vals.1, bf16[256,256]{1,0:T(8,128)(2,1)} %w1.1, bf16[256,256]{1,0:T(8,128)(2,1)} %w2.1, ...), custom_call_target="tpu_custom_call" | custom-call | flops 12884901888 | bytes 11534336 | tf_op jit(solution)/shard_map/whole/pallas_call | solution.py:414
  108.4 1.3 %copy.11 = bf16[2,2048,256]{2,1,0:T(8,128)(2,1)} copy(bf16[2,2048,256]{2,1,0:T(8,128)(2,1)S(1)} %bitcast.3) | data formatting | bytes 4194304
